TPU v7x, 128 devices: a whole 4x4x4 slice. The times are simulated.
128 devices in a mesh: pair: 8 (over x, core), row: 16 (over z, y).
Axes of the slice: x: 4, y: 4, z: 4, core: 2. Of those that a mesh axis runs over, the one named last changes fastest.
Arguments:
- descriptors: bfloat16 [64, 2048, 256], P('pair', 'row'), parts along dimension 0, may hold values from -8 to 8
- counts: int32 [64], P('pair'), parts along dimension 0, may hold values from 512 to 2048
- pairs: int32 [32, 2], P('pair'), parts along dimension 0, may hold values from 0 to 7, as said below
- bin_score: float32 [1], replicated, may hold values from 0.5 to 2
Outputs:
- log_match: float32 [32, 2048, 2048], P('pair', 'row'), parts along dimension 0
- row_bins: float32 [32, 2048], P('pair', 'row'), parts along dimension 0
- col_bins: float32 [32, 2048], P('pair'), parts along dimension 0
There are 8 independent parts, one for each index of `pair`. A program takes and returns all parts, laid end to end along the dimension named above; an argument that names none is the same for every part. Nothing has to cross between parts.
Inputs may be any that keep to these rules, and one draw needn't show every extreme that they name: Image k's keypoints are its first counts[k] slots. `pairs`: the two images of a pair differ.
All inputs are finite; a program needn't handle non-finite values.
Results may differ from a plain program's by a relative error of at most 0.0003.
Values may be sent and summed in bfloat16 or wider, within the bound.
A program may use at most 64 MiB of HBM per device.

v0:
```python
import jax
import jax.numpy as jnp
from jax import lax
from jax.sharding import Mesh
from jax.sharding import PartitionSpec as P

D = 256
ITERS = 10
ROW = ("row_0", "row_1")


NEG = -1e30


def all_in_one(x, axis):
    leaves = jax.tree.leaves(x)
    sequence = sorted(range(len(leaves)), key=lambda k: -leaves[k].size)
    width = (1, *leaves[sequence[0]].shape)[-1]
    lines = [
        jnp.pad(leaves[k].reshape(-1), (0, -leaves[k].size % width)).reshape(-1, width)
        for k in sequence
    ]
    both, at, found = (lax.all_gather(jnp.concatenate(lines), axis), 0, {})
    for k, line in zip(sequence, lines):
        share = both[:, at : at + len(line)].reshape(len(both), -1)
        found[k] = share[:, : leaves[k].size].reshape(-1, *leaves[k].shape)
        at += len(line)
    numbers = iter(range(len(leaves)))
    return jax.tree.map(lambda _: found[next(numbers)], x)


def joined_all(x, axes, combine):
    for axis in axes:
        pieces = all_in_one(x, axis)
        x = jax.tree.map(lambda part: part[0], pieces)
        for k in range(1, lax.axis_size(axis)):
            x = combine(x, jax.tree.map(lambda part: part[k], pieces))
    return x


def finish(peaks, totals, bin_extra):
    ceiling = jnp.maximum(peaks, bin_extra)
    return ceiling + jnp.log(totals * jnp.exp(peaks - ceiling) + jnp.exp(bin_extra - ceiling))


def merge_two(left_stats, right_stats):
    ceiling = jnp.maximum(left_stats[0], right_stats[0])
    summed = left_stats[1] * jnp.exp(left_stats[0] - ceiling) + right_stats[1] * jnp.exp(
        right_stats[0] - ceiling
    )
    return (ceiling, summed)


def combine_stats(left_stats, right_stats):
    peaks, totals = merge_two((left_stats[0], left_stats[1]), (right_stats[0], right_stats[1]))
    bin_peak, bin_total = merge_two(
        (left_stats[2], left_stats[3]), (right_stats[2], right_stats[3])
    )
    return (peaks, totals, bin_peak, bin_total)


def local_stats(shifted, kept, reduce_dim):
    peaks = jnp.max(shifted, axis=reduce_dim)
    totals = jnp.sum(
        jnp.where(kept, jnp.exp(shifted - jnp.expand_dims(peaks, reduce_dim)), 0.0), axis=reduce_dim
    )
    return (peaks, totals)


def on_device(descriptors, counts, pairs, bin_score):
    local_rows = descriptors.shape[1]
    all_cols = local_rows * lax.axis_size(ROW)
    score_scale = D ** (-0.5)
    offset = lax.axis_index(ROW) * local_rows
    row_desc = descriptors[pairs[:, 0]]
    col_desc = descriptors[pairs[:, 1]]
    n_rows = counts[pairs[:, 0]]
    n_cols = counts[pairs[:, 1]]
    bin_value = bin_score[0]
    scores = (
        jnp.einsum(
            "prd,pcd->prc",
            row_desc,
            lax.all_gather(col_desc, ROW, axis=1, tiled=True),
            preferred_element_type=jnp.float32,
        )
        * score_scale
    )
    row_index = offset + lax.iota(jnp.int32, local_rows)
    row_kept = row_index[None, :] < n_rows[:, None]
    col_kept = lax.iota(jnp.int32, all_cols)[None, :] < n_cols[:, None]
    row_count = n_rows.astype(jnp.float32)
    col_count = n_cols.astype(jnp.float32)
    log_norm = -jnp.log(row_count + col_count)
    mu_bin = jnp.log(col_count) + log_norm
    nu_bin = jnp.log(row_count) + log_norm

    def row_pass(col_pot, col_bin):
        shifted = jnp.where(col_kept[:, None, :], scores + col_pot[:, None, :], NEG)
        bin_edge = bin_value + col_bin
        peaks, totals = local_stats(shifted, col_kept[:, None, :], 2)
        row_pot = log_norm[:, None] - finish(peaks, totals, bin_edge[:, None])
        bin_line = jnp.where(col_kept, bin_value + col_pot, NEG)
        bin_peak, bin_total = local_stats(bin_line, col_kept, 1)
        row_bin = mu_bin - finish(bin_peak, bin_total, bin_edge)
        return (row_pot, row_bin)

    def column_pass(row_pot, row_bin):
        shifted = jnp.where(row_kept[:, :, None], scores + row_pot[:, :, None], NEG)
        edge_rows = jnp.where(row_kept, bin_value + row_pot, NEG)
        bin_extra = bin_value + row_bin
        peaks, totals = local_stats(shifted, row_kept[:, :, None], 1)
        bin_peak, bin_total = local_stats(edge_rows, row_kept, 1)
        peaks, totals, bin_peak, bin_total = joined_all(
            (peaks, totals, bin_peak, bin_total), ROW, combine_stats
        )
        col_pot = log_norm[:, None] - finish(peaks, totals, bin_extra[:, None])
        col_bin = nu_bin - finish(bin_peak, bin_total, bin_extra)
        return (col_pot, col_bin)

    def sweep(sweep_index, carried):
        row_pot, row_bin = row_pass(carried[0], carried[1])
        col_pot, col_bin = column_pass(row_pot, row_bin)
        return (col_pot, col_bin, row_pot, row_bin)

    pair_count = scores.shape[0]
    initial = (
        jnp.zeros((pair_count, all_cols), jnp.float32),
        jnp.zeros((pair_count,), jnp.float32),
        jnp.zeros((pair_count, local_rows), jnp.float32),
        jnp.zeros((pair_count,), jnp.float32),
    )
    col_pot, col_bin, row_pot, row_bin = lax.fori_loop(0, ITERS, sweep, initial)
    both_kept = row_kept[:, :, None] & col_kept[:, None, :]
    log_match = jnp.where(
        both_kept, scores + row_pot[:, :, None] + col_pot[:, None, :] - log_norm[:, None, None], 0.0
    )
    row_bins = jnp.where(row_kept, bin_value + row_pot + col_bin[:, None] - log_norm[:, None], 0.0)
    col_bins = jnp.where(col_kept, bin_value + row_bin[:, None] + col_pot - log_norm[:, None], 0.0)
    return (log_match, row_bins, col_bins)


def solution(mesh):
    finer = Mesh(mesh.devices.reshape(mesh.shape["pair"], 4, 4), ("pair", "row_0", "row_1"))
    in_specs = (P("pair", ROW, None), P("pair"), P("pair", None), P())
    out_specs = (P("pair", ROW, None), P("pair", ROW), P("pair", None))
    return jax.shard_map(
        on_device, mesh=finer, in_specs=in_specs, out_specs=out_specs, check_vma=False
    )
```

profile of v0, /device:TPU:0, one launch (start us, length us, event | category | flops | bytes accessed | tf_op | source)
XLA Modules:
  0.0 469.4 jit_solution(5412051058896793954)
XLA Ops:
  8.2 1.3 gather_fusion.3
  9.5 1.3 gather_fusion.1
  10.8 1.3 gather_fusion
  13.5 51.2 %all-gather.15.cloned.1.call-done = bf16[4,2048,256]{2,1,0:T(8,128)(2,1)} async-done(((bf16[4,128,256]{2,1,0:T(8,128)(2,1)}), bf16[4,2048,256]{2,1,0:T(8,128)(2,1)}) %all-gather.15.cloned.1.call-update) | async-done | bytes 4194320 | tf_op jit(solution)/shard_map/all_gather | solution.py:84
  64.7 5.7 %convolution_multiply_fusion = f32[4,128,2048]{2,1,0:T(8,128)} fusion(bf16[4,128,256]{2,1,0:T(8,128)(2,1)S(1)} %gather_fusion.2, bf16[4,2048,256]{2,1,0:T(8,128)(2,1)} %all-gather.15.cloned.1.call-done), kind=kOutput, calls=%fused_computation.143 | convolution fusion | flops 537919488 | bytes 8650752 | tf_op jit(solution)/shard_map/prd,pcd->prc/dot_general | solution.py:81
  70.4 384.2 %while.20 = (s32[]{:T(128)}, f32[4,2048]{1,0:T(4,128)S(1)}, f32[4]{0:T(128)S(1)}, f32[4,128]{1,0:T(4,128)}, f32[4]{0:T(128)}, /*index=5*/f32[4]{0:T(128)S(1)}, f...) while((s32[]{:T(128)}, f32[4,2048]{1,0:T(4,128)S(1)}, ...), condition=%wide.region_9.10_spmd.clone.clone, body=%wide.region_0.9_spmd.clone.sunk.clone | while | flops 17341648 | bytes 36197828 | solution.py:133
  71.5 3.0 fusion.103
  78.1 1.5 select_reduce_fusion.14
  80.5 13.0 %all-gather.11 = f32[4,10,2048]{2,1,0:T(8,128)S(1)} all-gather(f32[1,10,2048]{2,1,0:T(8,128)S(1)} %maximum_bitcast_fusion.6), channel_id=2, replica_groups=mesh['pair'=8,'row_0'=4,'row_1'=4] {'row_0'}, dimensions={0}, use_global_device_ids=true | all-gather | bytes 409600 | tf_op jit(solution)/shard_map/while/body/eval_jaxpr/all_gather | solution.py:23
  93.8 13.5 %all-gather.12 = f32[4,10,2048]{2,1,0:T(8,128)S(1)} all-gather(f32[1,10,2048]{2,1,0:T(8,128)S(1)} %maximum_bitcast_fusion.7), channel_id=3, replica_groups=mesh['pair'=8,'row_0'=4,'row_1'=4] {'row_1'}, dimensions={0}, use_global_device_ids=true | all-gather | bytes 409600 | tf_op jit(solution)/shard_map/while/body/eval_jaxpr/all_gather | solution.py:23
  110.7 3.0 fusion.103
  117.2 1.5 select_reduce_fusion.14
  119.6 12.8 %all-gather.11 = f32[4,10,2048]{2,1,0:T(8,128)S(1)} all-gather(f32[1,10,2048]{2,1,0:T(8,128)S(1)} %maximum_bitcast_fusion.6), channel_id=2, replica_groups=mesh['pair'=8,'row_0'=4,'row_1'=4] {'row_0'}, dimensions={0}, use_global_device_ids=true | all-gather | bytes 409600 | tf_op jit(solution)/shard_map/while/body/eval_jaxpr/all_gather | solution.py:23
  132.6 12.8 %all-gather.12 = f32[4,10,2048]{2,1,0:T(8,128)S(1)} all-gather(f32[1,10,2048]{2,1,0:T(8,128)S(1)} %maximum_bitcast_fusion.7), channel_id=3, replica_groups=mesh['pair'=8,'row_0'=4,'row_1'=4] {'row_1'}, dimensions={0}, use_global_device_ids=true | all-gather | bytes 409600 | tf_op jit(solution)/shard_map/while/body/eval_jaxpr/all_gather | solution.py:23
  148.8 3.0 fusion.103
  155.4 1.5 select_reduce_fusion.14
  157.7 12.8 %all-gather.11 = f32[4,10,2048]{2,1,0:T(8,128)S(1)} all-gather(f32[1,10,2048]{2,1,0:T(8,128)S(1)} %maximum_bitcast_fusion.6), channel_id=2, replica_groups=mesh['pair'=8,'row_0'=4,'row_1'=4] {'row_0'}, dimensions={0}, use_global_device_ids=true | all-gather | bytes 409600 | tf_op jit(solution)/shard_map/while/body/eval_jaxpr/all_gather | solution.py:23
  170.8 12.8 %all-gather.12 = f32[4,10,2048]{2,1,0:T(8,128)S(1)} all-gather(f32[1,10,2048]{2,1,0:T(8,128)S(1)} %maximum_bitcast_fusion.7), channel_id=3, replica_groups=mesh['pair'=8,'row_0'=4,'row_1'=4] {'row_1'}, dimensions={0}, use_global_device_ids=true | all-gather | bytes 409600 | tf_op jit(solution)/shard_map/while/body/eval_jaxpr/all_gather | solution.py:23
  186.9 3.0 fusion.103
  193.5 1.5 select_reduce_fusion.14
  195.9 12.8 %all-gather.11 = f32[4,10,2048]{2,1,0:T(8,128)S(1)} all-gather(f32[1,10,2048]{2,1,0:T(8,128)S(1)} %maximum_bitcast_fusion.6), channel_id=2, replica_groups=mesh['pair'=8,'row_0'=4,'row_1'=4] {'row_0'}, dimensions={0}, use_global_device_ids=true | all-gather | bytes 409600 | tf_op jit(solution)/shard_map/while/body/eval_jaxpr/all_gather | solution.py:23
  208.9 12.8 %all-gather.12 = f32[4,10,2048]{2,1,0:T(8,128)S(1)} all-gather(f32[1,10,2048]{2,1,0:T(8,128)S(1)} %maximum_bitcast_fusion.7), channel_id=3, replica_groups=mesh['pair'=8,'row_0'=4,'row_1'=4] {'row_1'}, dimensions={0}, use_global_device_ids=true | all-gather | bytes 409600 | tf_op jit(solution)/shard_map/while/body/eval_jaxpr/all_gather | solution.py:23
  225.1 3.0 fusion.103
  231.6 1.5 select_reduce_fusion.14
  234.0 12.8 %all-gather.11 = f32[4,10,2048]{2,1,0:T(8,128)S(1)} all-gather(f32[1,10,2048]{2,1,0:T(8,128)S(1)} %maximum_bitcast_fusion.6), channel_id=2, replica_groups=mesh['pair'=8,'row_0'=4,'row_1'=4] {'row_0'}, dimensions={0}, use_global_device_ids=true | all-gather | bytes 409600 | tf_op jit(solution)/shard_map/while/body/eval_jaxpr/all_gather | solution.py:23
  247.1 13.2 %all-gather.12 = f32[4,10,2048]{2,1,0:T(8,128)S(1)} all-gather(f32[1,10,2048]{2,1,0:T(8,128)S(1)} %maximum_bitcast_fusion.7), channel_id=3, replica_groups=mesh['pair'=8,'row_0'=4,'row_1'=4] {'row_1'}, dimensions={0}, use_global_device_ids=true | all-gather | bytes 409600 | tf_op jit(solution)/shard_map/while/body/eval_jaxpr/all_gather | solution.py:23
  263.6 3.0 fusion.103
  270.2 1.5 select_reduce_fusion.14
  272.6 12.8 %all-gather.11 = f32[4,10,2048]{2,1,0:T(8,128)S(1)} all-gather(f32[1,10,2048]{2,1,0:T(8,128)S(1)} %maximum_bitcast_fusion.6), channel_id=2, replica_groups=mesh['pair'=8,'row_0'=4,'row_1'=4] {'row_0'}, dimensions={0}, use_global_device_ids=true | all-gather | bytes 409600 | tf_op jit(solution)/shard_map/while/body/eval_jaxpr/all_gather | solution.py:23
  285.6 13.5 %all-gather.12 = f32[4,10,2048]{2,1,0:T(8,128)S(1)} all-gather(f32[1,10,2048]{2,1,0:T(8,128)S(1)} %maximum_bitcast_fusion.7), channel_id=3, replica_groups=mesh['pair'=8,'row_0'=4,'row_1'=4] {'row_1'}, dimensions={0}, use_global_device_ids=true | all-gather | bytes 409600 | tf_op jit(solution)/shard_map/while/body/eval_jaxpr/all_gather | solution.py:23
  302.4 3.0 fusion.103
  309.0 1.5 select_reduce_fusion.14
  311.4 12.8 %all-gather.11 = f32[4,10,2048]{2,1,0:T(8,128)S(1)} all-gather(f32[1,10,2048]{2,1,0:T(8,128)S(1)} %maximum_bitcast_fusion.6), channel_id=2, replica_groups=mesh['pair'=8,'row_0'=4,'row_1'=4] {'row_0'}, dimensions={0}, use_global_device_ids=true | all-gather | bytes 409600 | tf_op jit(solution)/shard_map/while/body/eval_jaxpr/all_gather | solution.py:23
  324.4 13.1 %all-gather.12 = f32[4,10,2048]{2,1,0:T(8,128)S(1)} all-gather(f32[1,10,2048]{2,1,0:T(8,128)S(1)} %maximum_bitcast_fusion.7), channel_id=3, replica_groups=mesh['pair'=8,'row_0'=4,'row_1'=4] {'row_1'}, dimensions={0}, use_global_device_ids=true | all-gather | bytes 409600 | tf_op jit(solution)/shard_map/while/body/eval_jaxpr/all_gather | solution.py:23
  340.9 3.0 fusion.103
  347.5 1.5 select_reduce_fusion.14
  349.8 13.2 %all-gather.11 = f32[4,10,2048]{2,1,0:T(8,128)S(1)} all-gather(f32[1,10,2048]{2,1,0:T(8,128)S(1)} %maximum_bitcast_fusion.6), channel_id=2, replica_groups=mesh['pair'=8,'row_0'=4,'row_1'=4] {'row_0'}, dimensions={0}, use_global_device_ids=true | all-gather | bytes 409600 | tf_op jit(solution)/shard_map/while/body/eval_jaxpr/all_gather | solution.py:23
  363.3 12.8 %all-gather.12 = f32[4,10,2048]{2,1,0:T(8,128)S(1)} all-gather(f32[1,10,2048]{2,1,0:T(8,128)S(1)} %maximum_bitcast_fusion.7), channel_id=3, replica_groups=mesh['pair'=8,'row_0'=4,'row_1'=4] {'row_1'}, dimensions={0}, use_global_device_ids=true | all-gather | bytes 409600 | tf_op jit(solution)/shard_map/while/body/eval_jaxpr/all_gather | solution.py:23
  379.5 3.0 fusion.103
  386.0 1.5 select_reduce_fusion.14
  388.4 12.8 %all-gather.11 = f32[4,10,2048]{2,1,0:T(8,128)S(1)} all-gather(f32[1,10,2048]{2,1,0:T(8,128)S(1)} %maximum_bitcast_fusion.6), channel_id=2, replica_groups=mesh['pair'=8,'row_0'=4,'row_1'=4] {'row_0'}, dimensions={0}, use_global_device_ids=true | all-gather | bytes 409600 | tf_op jit(solution)/shard_map/while/body/eval_jaxpr/all_gather | solution.py:23
  401.5 12.8 %all-gather.12 = f32[4,10,2048]{2,1,0:T(8,128)S(1)} all-gather(f32[1,10,2048]{2,1,0:T(8,128)S(1)} %maximum_bitcast_fusion.7), channel_id=3, replica_groups=mesh['pair'=8,'row_0'=4,'row_1'=4] {'row_1'}, dimensions={0}, use_global_device_ids=true | all-gather | bytes 409600 | tf_op jit(solution)/shard_map/while/body/eval_jaxpr/all_gather | solution.py:23
  417.6 3.0 fusion.103
  424.2 1.5 select_reduce_fusion.14
  426.5 12.8 %all-gather.11 = f32[4,10,2048]{2,1,0:T(8,128)S(1)} all-gather(f32[1,10,2048]{2,1,0:T(8,128)S(1)} %maximum_bitcast_fusion.6), channel_id=2, replica_groups=mesh['pair'=8,'row_0'=4,'row_1'=4] {'row_0'}, dimensions={0}, use_global_device_ids=true | all-gather | bytes 409600 | tf_op jit(solution)/shard_map/while/body/eval_jaxpr/all_gather | solution.py:23
  439.6 12.8 %all-gather.12 = f32[4,10,2048]{2,1,0:T(8,128)S(1)} all-gather(f32[1,10,2048]{2,1,0:T(8,128)S(1)} %maximum_bitcast_fusion.7), channel_id=3, replica_groups=mesh['pair'=8,'row_0'=4,'row_1'=4] {'row_1'}, dimensions={0}, use_global_device_ids=true | all-gather | bytes 409600 | tf_op jit(solution)/shard_map/while/body/eval_jaxpr/all_gather | solution.py:23
  456.0 1.3 subtract_select_fusion.2
  457.3 5.2 %subtract_select_fusion = f32[4,128,2048]{2,1,0:T(8,128)} fusion(f32[4,128,2048]{2,1,0:T(8,128)} %get-tuple-element.446, f32[4]{0:T(128)S(1)} %get-tuple-element.451, f32[4,2048]{1,0:T(4,128)S(1)} %get-tuple-element.148, f32[4,128]{1,0:T(4,128)} %get-tuple-element.147, pred[4,2048]{1,0:T(4,128)(4,1)S(1)} %iota_compare_fusion.1, ...), kind=kLoop, calls=%fused_computation.142 | loop fusion | flops 5242880 | bytes 8432144 | tf_op jit(solution)/shard_map/jit(_where)/select_n | solution.py:135
  (287 shorter events, 82.6 us)
Async XLA Ops:
  7.2 1.1 copy-start
  7.2 57.6 %all-gather.15.cloned.1.call-start = ((), (), s32[]{:S(2)}) async-start(), calls=%async_computation | async-start | bytes 4456448 | tf_op jit(solution)/shard_map/all_gather | solution.py:84
  70.4 4.1 copy-start.1
  77.3 2.3 copy-start.2
  109.6 4.1 copy-start.1
  116.4 2.3 copy-start.2
  147.7 4.1 copy-start.1
  154.6 2.3 copy-start.2
  185.8 4.1 copy-start.1
  192.7 2.3 copy-start.2
  224.0 4.1 copy-start.1
  230.8 2.3 copy-start.2
  262.5 4.1 copy-start.1
  269.4 2.3 copy-start.2
  301.3 4.1 copy-start.1
  308.2 2.3 copy-start.2
  339.8 4.1 copy-start.1
  346.7 2.3 copy-start.2
  378.4 4.1 copy-start.1
  385.2 2.3 copy-start.2
  416.5 4.1 copy-start.1
  423.4 2.3 copy-start.2
Sparse Core Ops, SparseCore 0:
  10.7 53.9 all-gather.14
where the time goes:
time: 470 us; the launch traced here: 469 us
  blocking collectives  259 us (55%)
  other arithmetic  131 us (28%)
  waiting for transfers between devices  51.3 us (11%)
  between operations  14.8 us (3%)
  local copies, waits for them, and re-layouts  6.37 us (1%)
  matrix products  5.7 us (1%)
    all_gather x20, blocking collectives, all_in_one(): both, at, found = (lax.all_gather(jnp.concatenate(lines), axis), 0, {})  259 us
    reduce_max x40, other arithmetic, local_stats(): peaks = jnp.max(shifted, axis=reduce_dim)  56.1 us
    all_gather x1, waiting for transfers between devices, on_device(): lax.all_gather(col_desc, ROW, axis=1, tiled=True)  51.2 us
    reduce_sum x40, other arithmetic, local_stats(): jnp.sum(jnp.where(kept, jnp.exp(shifted - jnp.expand_dims(peaks, reduce_d...  44 us
    sub x10, other arithmetic, column_pass(): col_bin = nu_bin - finish(bin_peak, bin_total, bin_extra)  11.8 us
  transfers between devices with their start and end apart: 1, of which 1 were waited for; matrix products, arithmetic and copies ran while one was open for 1% of the time, Pallas kernels for 0%

commit v1 on v0

v1 whole, which is shorter than its diff:
```python
import functools

import jax
import jax.numpy as jnp
from jax import lax
from jax.experimental import pallas as pl
from jax.experimental.pallas import tpu as pltpu
from jax.sharding import Mesh
from jax.sharding import PartitionSpec as P

D = 256
ITERS = 10
KP = 2048
B = 128
W = KP + 128
CHUNKS = W // 128
RB = 256
STEPS = KP // RB
EXACT = 2
LOG2E = 1.4426950408889634
LN2 = 0.6931471805599453
SHIFT = 65.0
NEG = -1e30
UVROWS = 24
MESH = pl.DeviceIdType.MESH
F32 = jnp.float32
BF16 = jnp.bfloat16
TRANS = (((1,), (1,)), ((), ()))


def remote(src, dst, send, recv, z, y):
    return pltpu.make_async_remote_copy(
        src_ref=src, dst_ref=dst, send_sem=send, recv_sem=recv,
        device_id={"z": z, "y": y}, device_id_type=MESH,
    )


class Gather:
    def __init__(self, cols, send, recv, z, y):
        self.cols, self.send, self.recv, self.at = cols, send, recv, (z, y)

    def where(self, route, first, second):
        return (first, second) if route == 0 else (second, first)

    def part(self, route, which):
        lo = 2 * route
        return {"both": pl.ds(lo, 2), "low": pl.ds(lo, 1), "high": pl.ds(lo + 1, 1)}[which]

    def block(self, route, which, first, second):
        z, y = self.where(route, first, second)
        return self.cols.at[self.part(route, which), z, pl.ds(pl.multiple_of(y * B, B), B), :]

    def line(self, route, which, second):
        part = self.part(route, which)
        if route == 0:
            return self.cols.at[part, :, pl.ds(pl.multiple_of(second * B, B), B), :]
        return self.cols.at[part, second, :, :]

    def copy(self, route, step, sign, k, sending):
        f, g = self.at if route == 0 else self.at[::-1]
        slot = route * 14 + {1: 0, 2: 2, 3: 4, 4: 12}[step] + (sign < 0)
        if step == 3:
            slot += 2 * k
        wrap = lambda a: lax.rem(a + 8, 4)
        if step == 1:
            ref = self.block(route, "both", f if sending else wrap(f - sign), g)
        elif step == 2:
            ref = self.block(route, "low" if sign > 0 else "high", wrap(f - sign) if sending else wrap(f + 2), g)
        elif step == 3:
            ref = self.block(route, "both", wrap(f + k), g if sending else wrap(g - sign))
        else:
            ref = self.line(route, "low" if sign > 0 else "high", wrap(g - sign) if sending else wrap(g + 2))
        if step <= 2:
            z, y = self.where(route, wrap(f + sign), g)
        else:
            z, y = self.where(route, f, wrap(g + sign))
        return remote(ref, ref, self.send.at[slot], self.recv.at[slot], z, y)

    def start(self, step, ks=(0,)):
        for k in ks:
            for route in (0, 1):
                for sign in (1, -1):
                    self.copy(route, step, sign, k, True).start()

    def arrive(self, step, ks=(0,)):
        for k in ks:
            for route in (0, 1):
                for sign in (1, -1):
                    self.copy(route, step, sign, k, False).wait_recv()

    def sent(self, step, ks=(0,)):
        for k in ks:
            for route in (0, 1):
                for sign in (1, -1):
                    self.copy(route, step, sign, k, True).wait_send()

    def point(self, number):
        if number == 0:
            self.start(1)
            self.start(3, (0,))
        elif number == 1:
            self.arrive(1)
            self.start(2)
            self.start(3, (1, 3))
        elif number == 2:
            self.arrive(2)
            self.start(3, (2,))
        elif number == 3:
            self.arrive(3, (0, 1, 3, 2))
            self.start(4)
        else:
            self.arrive(4)

    def drain(self):
        self.sent(1)
        self.sent(2)
        self.sent(3, (0, 1, 2, 3))
        self.sent(4)


def count_vector(counts, pairs, p, side):
    return jnp.full((1, 128), counts[pairs[p, side]], jnp.int32)


def lanes():
    return lax.broadcasted_iota(jnp.int32, (1, 128), 1)


def main_kernel(
    pairs, counts, bins, desc, s_out, uv_out,
    sel, own, cols, kmat, khigh, klow, ys, nus, acc, xs, xv, mv, stage, uvr, sv,
    a_send, a_recv, g_send, g_recv, u_send, u_recv, o_sem,
):
    z, y = lax.axis_index("z"), lax.axis_index("y")
    core = lax.rem(lax.axis_index("pair"), 2)
    me = z * 4 + y
    mine = pl.ds(pl.multiple_of(me * B, B), B)

    barrier = pltpu.get_barrier_semaphore()
    for other in range(1, 16):
        pl.semaphore_signal(
            barrier, inc=1, device_id_type=MESH,
            device_id={"z": lax.rem(z + other // 4, 4), "y": lax.rem(y + other % 4, 4)},
        )
    owner_y = [lax.rem(p + 2 * core, 4) for p in range(4)]
    owner = y == lax.rem(z + 2 * core, 4)

    for p in range(4):
        sel[p, 0] = desc[pairs[p, 0]]
        col = desc[pairs[p, 1]]
        sel[p, 1] = col
        cols[p, z, pl.ds(pl.multiple_of(y * B, B), B), :] = col

    @pl.when(owner)
    def _():
        own[0, mine, :] = desc[pairs[z, 0]]
        own[1, mine, :] = desc[pairs[z, 1]]

    pl.semaphore_wait(barrier, 15)

    def to_owner(p):
        there = own.at[:, mine, :]
        return remote(sel.at[p], there, a_send.at[p], a_recv.at[me], p, owner_y[p])

    for p in range(4):
        pl.when(jnp.logical_not((z == p) & (y == owner_y[p])))(lambda p=p: to_owner(p).start())
    for p in range(4):
        pl.when(jnp.logical_not((z == p) & (y == owner_y[p])))(lambda p=p: to_owner(p).wait_send())

    gather = Gather(cols, g_send, g_recv, z, y)
    gather.point(0)

    @pl.when(jnp.logical_not(owner))
    def _():
        for number in range(1, 5):
            gather.point(number)

    @pl.when(owner)
    def _():
        for source in range(16):
            def landed(source=source):
                there = own.at[:, pl.ds(source * B, B), :]
                remote(there, there, a_send.at[0], a_recv.at[source], z, y).wait_recv()
            pl.when(me != source)(landed)

        na, nb = count_vector(counts, pairs, z, 0), count_vector(counts, pairs, z, 1)
        naf, nbf = na.astype(F32), nb.astype(F32)
        one = 1.0 / (naf + nbf)
        bin_value = jnp.full((1, 128), bins[0], F32)
        bin_two = bin_value * LOG2E
        for c in range(16):
            kept = lanes() + c * 128 < nb
            nus[:, c * 128 : c * 128 + 128] = jnp.where(kept, one, 0.0)
            ys[:, c * 128 : c * 128 + 128] = jnp.where(kept, 1.0, 0.0)
        nus[:, KP:W] = jnp.where(lanes() == 0, naf * one, 0.0)
        ys[:, KP:W] = jnp.where(lanes() == 0, 1.0, 0.0)
        mu_bin = nbf * one

        def score_step(b, _):
            rows = pl.ds(pl.multiple_of(b * RB, RB), RB)
            left = own[0, rows, :]
            top = jnp.broadcast_to(bin_two, (RB, 128))
            for c in range(8):
                part = lax.dot_general(left, own[1, c * 256 : c * 256 + 256, :], TRANS, preferred_element_type=F32)
                for h in range(2):
                    at = c * 256 + h * 128
                    veil = jnp.where(lanes() + at < nb, 0.0, NEG)
                    piece = part[:, h * 128 : h * 128 + 128] * (LOG2E / 16.0) + veil
                    kmat[rows, at : at + 128] = piece
                    top = jnp.maximum(top, piece)
            top = jnp.broadcast_to(jnp.max(top, axis=1, keepdims=True), (RB, 128)) - SHIFT
            for h in range(2):
                mv[pl.ds(2 * b + h, 1), :] = top[h * 128 : h * 128 + 128].T[0:1, :]
            for c in range(CHUNKS):
                at = slice(c * 128, c * 128 + 128)
                if c < 16:
                    value = jnp.exp2(kmat[rows, at] - top)
                else:
                    value = jnp.where(lanes() == 0, jnp.exp2(bin_two - top), 0.0)
                kmat[rows, at] = value
                high = value.astype(BF16)
                khigh[rows, at] = high
                klow[rows, at] = (value - high.astype(F32)).astype(BF16)
            return 0

        lax.fori_loop(0, STEPS, score_step, 0)
        gather.point(1)

        def row_step(b):
            for h in range(2):
                rows = pl.ds(pl.multiple_of(b * RB + h * 128, 128), 128)
                total = kmat[rows, 0:128] * ys[:, 0:128]
                for c in range(1, CHUNKS):
                    total += kmat[rows, c * 128 : c * 128 + 128] * ys[:, c * 128 : c * 128 + 128]
                x = one / jnp.sum(total.T, axis=0, keepdims=True)
                xv[pl.ds(2 * b + h, 1), :] = x
                x = jnp.where(lanes() + (b * RB + h * 128) < na, x, 0.0)
                high = x.astype(BF16).astype(F32)
                line = lax.broadcasted_iota(jnp.int32, (16, 128), 0)
                both = jnp.where(line == 0, high, jnp.where(line == 1, x - high, 0.0))
                xs[lax.rem(b, 2), :, h * 128 : h * 128 + 128] = both.astype(BF16)

        def col_step(b, exact):
            rows = pl.ds(pl.multiple_of(b * RB, RB), RB)
            x = xs[lax.rem(b, 2)]
            total = jnp.dot(x, khigh[rows, :], preferred_element_type=F32)
            if exact:
                total += jnp.dot(x, klow[rows, :], preferred_element_type=F32)
            acc[...] += total

        def sweep(exact):
            spread = jnp.sum(ys[...], axis=1, keepdims=True)
            x_bin = mu_bin / jnp.broadcast_to(spread, (1, 128))
            stage[0, 17:18, :] = x_bin
            acc[...] = jnp.zeros_like(acc)
            row_step(0)

            def both(b, _):
                row_step(b)
                col_step(b - 1, exact)
                return 0

            lax.fori_loop(1, STEPS, both, 0)
            col_step(STEPS - 1, exact)
            for c in range(CHUNKS):
                at = slice(c * 128, c * 128 + 128)
                ys[:, at] = nus[:, at] / (acc[0:1, at] + acc[1:2, at] + x_bin)

        def early(i, _):
            sweep(False)
            pl.when(i == 2)(lambda: gather.point(2))
            pl.when(i == 5)(lambda: gather.point(3))
            return 0

        lax.fori_loop(0, ITERS - EXACT, early, 0)
        lax.fori_loop(0, EXACT, lambda i, _: (sweep(True), 0)[1], 0)

        u = jnp.log(xv[...]) - mv[...] * LN2
        u_bin = jnp.log(stage[0, 17:18, :]) - bin_value
        v = [jnp.log(ys[:, c * 128 : c * 128 + 128]) for c in range(16)]
        v_bin = jnp.log(jnp.broadcast_to(ys[:, KP : KP + 1], (1, 128)))
        for d in range(16):
            for c in range(16):
                stage[d, c : c + 1, :] = v[c]
            stage[d, 16:17, :] = u[d : d + 1, :]
            stage[d, 17:18, :] = u_bin
            stage[d, 18:19, :] = v_bin
            stage[d, 19:24, :] = jnp.zeros((5, 128), F32)

        uvr[z] = stage[me]
        for d in range(16):
            def send(d=d):
                remote(stage.at[d], uvr.at[z], u_send.at[d], u_recv.at[z], d // 4, d % 4).start()
            pl.when(me != d)(send)
        gather.point(4)

    for p in range(4):
        for c in range(8):
            part = lax.dot_general(
                sel[p, 0], cols[p, c // 2, (c % 2) * 256 : (c % 2) * 256 + 256, :], TRANS, preferred_element_type=F32
            )
            sv[p, :, c * 256 : c * 256 + 256] = part * 0.0625
        pltpu.make_async_copy(sv.at[p], s_out.at[p], o_sem.at[p]).start()
    gather.drain()
    for p in range(4):
        def landed(p=p):
            remote(uvr.at[p], uvr.at[p], u_send.at[0], u_recv.at[p], z, y).wait_recv()
        pl.when(jnp.logical_not((z == p) & (y == owner_y[p])))(landed)
    uv_out[...] = uvr[...]

    @pl.when(owner)
    def _():
        for d in range(16):
            def gone(d=d):
                remote(stage.at[d], uvr.at[z], u_send.at[d], u_recv.at[z], d // 4, d % 4).wait_send()
            pl.when(me != d)(gone)

    for p in range(4):
        pltpu.make_async_copy(sv.at[p], s_out.at[p], o_sem.at[p]).wait()


def last_kernel(pairs, counts, bins, s, uv, out, row_out, col_out):
    p = pl.program_id(0)
    start = (lax.axis_index("z") * 4 + lax.axis_index("y")) * B
    na, nb = count_vector(counts, pairs, p, 0), count_vector(counts, pairs, p, 1)
    norm = -jnp.log((na + nb).astype(F32))
    bin_value = jnp.full((1, 128), bins[0], F32)
    u = uv[p, 16:17, :]
    row_kept = lanes() + start < na
    u_down = jnp.broadcast_to(u, (B, 128)).T
    kept = lax.broadcasted_iota(jnp.int32, (B, 128), 0) + start < na
    for c in range(16):
        at = slice(c * 128, c * 128 + 128)
        v = uv[p, c : c + 1, :]
        col_kept = lanes() + c * 128 < nb
        out[0, :, at] = jnp.where(kept & col_kept, s[0, :, at] + u_down + v - norm, 0.0)

    def bin_lines(q):
        row_out[q : q + 1, :] = jnp.where(row_kept, bin_value + u + uv[p, 18:19, :] - norm, 0.0)
        for c in range(16):
            line = bin_value + uv[p, 17:18, :] + uv[p, c : c + 1, :] - norm
            col_out[q : q + 1, c * 128 : c * 128 + 128] = jnp.where(lanes() + c * 128 < nb, line, 0.0)

    for q in range(4):
        pl.when(p == q)(lambda q=q: bin_lines(q))


def on_device(descriptors, counts, pairs, bin_score):
    smem = pl.BlockSpec(memory_space=pltpu.SMEM)
    vmem = pl.BlockSpec(memory_space=pltpu.VMEM)
    dma = pltpu.SemaphoreType.DMA
    s, uv = pl.pallas_call(
        main_kernel,
        out_shape=(
            jax.ShapeDtypeStruct((4, B, KP), F32),
            jax.ShapeDtypeStruct((4, UVROWS, 128), F32),
        ),
        in_specs=[smem, smem, smem, vmem],
        out_specs=(pl.BlockSpec(memory_space=pl.ANY), vmem),
        scratch_shapes=[
            pltpu.VMEM((4, 2, B, D), BF16),
            pltpu.VMEM((2, KP, D), BF16),
            pltpu.VMEM((4, 4, 4 * B, D), BF16),
            pltpu.VMEM((KP, W), F32),
            pltpu.VMEM((KP, W), BF16),
            pltpu.VMEM((KP, W), BF16),
            pltpu.VMEM((1, W), F32),
            pltpu.VMEM((1, W), F32),
            pltpu.VMEM((16, W), F32),
            pltpu.VMEM((2, 16, RB), BF16),
            pltpu.VMEM((16, 128), F32),
            pltpu.VMEM((16, 128), F32),
            pltpu.VMEM((16, UVROWS, 128), F32),
            pltpu.VMEM((4, UVROWS, 128), F32),
            pltpu.VMEM((4, B, KP), F32),
            dma((4,)), dma((16,)), dma((28,)), dma((28,)), dma((16,)), dma((4,)), dma((4,)),
        ],
        compiler_params=pltpu.CompilerParams(
            collective_id=0, has_side_effects=True, vmem_limit_bytes=60 * 1024 * 1024
        ),
        name="match",
    )(pairs, counts, bin_score, descriptors)
    return pl.pallas_call(
        last_kernel,
        grid=(4,),
        out_shape=(
            jax.ShapeDtypeStruct((4, B, KP), F32),
            jax.ShapeDtypeStruct((4, B), F32),
            jax.ShapeDtypeStruct((4, KP), F32),
        ),
        in_specs=[
            smem, smem, smem,
            pl.BlockSpec((1, B, KP), lambda p: (p, 0, 0)),
            pl.BlockSpec((4, UVROWS, 128), lambda p: (0, 0, 0)),
        ],
        out_specs=(
            pl.BlockSpec((1, B, KP), lambda p: (p, 0, 0)),
            pl.BlockSpec((4, B), lambda p: (0, 0)),
            pl.BlockSpec((4, KP), lambda p: (0, 0)),
        ),
        name="assign",
    )(pairs, counts, bin_score, s, uv)


def solution(mesh):
    finer = Mesh(mesh.devices.reshape(mesh.shape["pair"], 4, 4), ("pair", "z", "y"))
    row = ("z", "y")
    return jax.shard_map(
        on_device,
        mesh=finer,
        in_specs=(P("pair", row, None), P("pair"), P("pair", None), P()),
        out_specs=(P("pair", row, None), P("pair", row), P("pair", None)),
        check_vma=False,
    )
```

time: 470 us -> 86.5 us (0.18)
  blocking collectives: 259 us -> 0 us
  other arithmetic: 131 us -> 0 us
  Pallas kernels: 0 us -> 83.6 us
  waiting for transfers between devices: 51.3 us -> 0 us
  between operations: 14.8 us -> 1.29 us
  matrix products: 5.7 us -> 0 us
  local copies, waits for them, and re-layouts: 6.37 us -> 1.34 us
    all_gather x20 -> x0, blocking collectives: 259 us -> none  [all_in_one(): both, at, found = (lax.all_gather(jnp.concatenate(lines), axis), 0, {})]
    pallas_call x0 -> x2, Pallas kernels: none -> 83.6 us  [the longest x1 78.4 us: on_device(): pl.pallas_call(main_kernel, out_shape=(jax.ShapeDtypeStruct((4, B, KP), F...]
    reduce_max x40 -> x0, other arithmetic: 56.1 us -> none  [local_stats(): peaks = jnp.max(shifted, axis=reduce_dim)]
    all_gather x1 -> x0, waiting for transfers between devices: 51.2 us -> none  [on_device(): lax.all_gather(col_desc, ROW, axis=1, tiled=True)]
    reduce_sum x40 -> x0, other arithmetic: 44 us -> none  [local_stats(): jnp.sum(jnp.where(kept, jnp.exp(shifted - jnp.expand_dims(peaks, reduce_d...]
    sub x20 -> x0, other arithmetic: 13.1 us -> none  [the longest x10 11.8 us: column_pass(): col_bin = nu_bin - finish(bin_peak, bin_total, bin_extra)]
    add x33 -> x0, other arithmetic: 8.31 us -> none  [the longest x10 6.53 us: row_pass(): bin_edge = bin_value + col_bin]
    select_n x4 -> x0, other arithmetic: 7.96 us -> none  [the longest x1 5.18 us: on_device(): jnp.where(both_kept, scores + row_pot[:, :, None] + col_pot[:, None, :] -...]
  transfers between devices with their start and end apart: 1 -> 0, of which waited for: 1 -> 0; matrix products, arithmetic and copies ran while one was open for 1% -> 0% of each run, Pallas kernels for 0% -> 0%
where the time goes in v1:
time: 86.5 us; the launch traced here: 86.2 us
  Pallas kernels  83.6 us (97%)
  local copies, waits for them, and re-layouts  1.34 us (2%)
  between operations  1.29 us (1%)
    pallas_call x1, Pallas kernels, on_device(): pl.pallas_call(main_kernel, out_shape=(jax.ShapeDtypeStruct((4, B, KP), F...  78.4 us
    pallas_call x1, Pallas kernels, on_device(): pl.pallas_call(last_kernel, grid=(4,), out_shape=(jax.ShapeDtypeStruct((4...  5.14 us

profile of v1, /device:TPU:0, one launch (start us, length us, event | category | flops | bytes accessed | tf_op | source)
XLA Modules:
  0.0 86.2 jit_solution(8613464970024678949)
XLA Ops:
  1.3 1.3 %copy.8.pairs = s32[4,2]{1,0:T(4,128)} copy(s32[4,2]{0,1:T(2,128)} %param.6) | data formatting | bytes 64 | tf_op args[2]
  2.6 78.4 %match.1 = (f32[4,128,2048]{2,1,0:T(8,128)}, f32[4,24,128]{2,1,0:T(8,128)}) custom-call(s32[4,2]{1,0:T(4,128)} %copy.8.pairs, s32[8]{0:T(128)} %counts.3, f32[1]{0:T(128)S(6)} %copy.9.bins, bf16[8,128,256]{2,1,0:T(8,128)(2,1)} %desc.1), custom_call_target="tpu_custom_call" | custom-call | tf_op jit(solution)/shard_map/match/pallas_call | solution.py:352
  81.1 5.1 %assign.1 = (f32[4,128,2048]{2,1,0:T(8,128)}, f32[4,128]{1,0:T(4,128)}, f32[4,2048]{1,0:T(4,128)}) custom-call(s32[4,2]{1,0:T(4,128)} %copy.8.pairs, s32[8]{0:T(128)} %counts.3, f32[1]{0:T(128)S(6)} %copy.9.bins, f32[4,128,2048]{2,1,0:T(8,128)} %get-tuple-element.5.s, f32[4,24,128]{2,1,0:T(8,128)} %get-tuple-element.6.uv), custom_call_target="tpu_custom_call" | custom-call | tf_op jit(solution)/shard_map/assign/pallas_call | solution.py:383

commit v2 on v1

v2 whole, which is shorter than its diff:
```python
import contextlib

import jax
import jax.numpy as jnp
from jax import lax
from jax.experimental import pallas as pl
from jax.experimental.pallas import tpu as pltpu
from jax.sharding import Mesh
from jax.sharding import PartitionSpec as P

D = 256
ITERS = 10
KP = 2048
B = 128
W = KP + 128
CHUNKS = W // 128
RB = 256
STEPS = KP // RB
EXACT = 2
LOG2E = 1.4426950408889634
LN2 = 0.6931471805599453
SHIFT = 65.0
NEG = -1e30
UVROWS = 24
MESH = pl.DeviceIdType.MESH
SCOPES = False
EAGER = True
F32 = jnp.float32
BF16 = jnp.bfloat16
TRANS = (((1,), (1,)), ((), ()))


def scope(name):
    return jax.named_scope(name) if SCOPES else contextlib.nullcontext()


def remote(src, dst, send, recv, z, y):
    return pltpu.make_async_remote_copy(
        src_ref=src, dst_ref=dst, send_sem=send, recv_sem=recv,
        device_id={"z": z, "y": y}, device_id_type=MESH,
    )


class Gather:
    def __init__(self, cols, send, recv, z, y):
        self.cols, self.send, self.recv, self.at = cols, send, recv, (z, y)

    def where(self, route, first, second):
        return (first, second) if route == 0 else (second, first)

    def part(self, route, which):
        lo = 2 * route
        return {"both": pl.ds(lo, 2), "low": pl.ds(lo, 1), "high": pl.ds(lo + 1, 1)}[which]

    def block(self, route, which, first, second):
        z, y = self.where(route, first, second)
        return self.cols.at[self.part(route, which), z, pl.ds(pl.multiple_of(y * B, B), B), :]

    def line(self, route, which, second):
        part = self.part(route, which)
        if route == 0:
            return self.cols.at[part, :, pl.ds(pl.multiple_of(second * B, B), B), :]
        return self.cols.at[part, second, :, :]

    def copy(self, route, step, sign, k, sending):
        f, g = self.at if route == 0 else self.at[::-1]
        slot = route * 14 + {1: 0, 2: 2, 3: 4, 4: 12}[step] + (sign < 0)
        if step == 3:
            slot += 2 * k
        wrap = lambda a: lax.rem(a + 8, 4)
        if step == 1:
            ref = self.block(route, "both", f if sending else wrap(f - sign), g)
        elif step == 2:
            ref = self.block(route, "low" if sign > 0 else "high", wrap(f - sign) if sending else wrap(f + 2), g)
        elif step == 3:
            ref = self.block(route, "both", wrap(f + k), g if sending else wrap(g - sign))
        else:
            ref = self.line(route, "low" if sign > 0 else "high", wrap(g - sign) if sending else wrap(g + 2))
        if step <= 2:
            z, y = self.where(route, wrap(f + sign), g)
        else:
            z, y = self.where(route, f, wrap(g + sign))
        return remote(ref, ref, self.send.at[slot], self.recv.at[slot], z, y)

    def start(self, step, ks=(0,)):
        for k in ks:
            for route in (0, 1):
                for sign in (1, -1):
                    self.copy(route, step, sign, k, True).start()

    def arrive(self, step, ks=(0,)):
        for k in ks:
            for route in (0, 1):
                for sign in (1, -1):
                    self.copy(route, step, sign, k, False).wait_recv()

    def sent(self, step, ks=(0,)):
        for k in ks:
            for route in (0, 1):
                for sign in (1, -1):
                    self.copy(route, step, sign, k, True).wait_send()

    def point(self, number):
        if number == 0:
            self.start(1)
            self.start(3, (0,))
        elif number == 1:
            self.arrive(1)
            self.start(2)
            self.start(3, (1, 3))
        elif number == 2:
            self.arrive(2)
            self.start(3, (2,))
        elif number == 3:
            self.arrive(3, (0, 1, 3, 2))
            self.start(4)
        else:
            self.arrive(4)

    def drain(self):
        self.sent(1)
        self.sent(2)
        self.sent(3, (0, 1, 2, 3))
        self.sent(4)


def count_vector(counts, pairs, p, side):
    return jnp.full((1, 128), counts[pairs[side, p]], jnp.int32)


def lanes():
    return lax.broadcasted_iota(jnp.int32, (1, 128), 1)


NEAR = (
    (0, 0), (0, 1), (0, 3), (1, 0), (3, 0), (1, 1), (1, 3), (3, 1), (3, 3), (0, 2), (2, 0), (1, 2), (3, 2), (2, 1), (2, 3), (2, 2),
)


def main_kernel(
    pairs, counts, bins, desc, s_out, uv_out,
    sel, own, cols, kmat, khigh, raw0, raw1, top0, top1, ys, nus, xd, xv, mv, stage, uvr, sv,
    a_send, c_recv, r_recv, g_send, g_recv, u_send, u_recv, o_sem,
):
    z, y = lax.axis_index("z"), lax.axis_index("y")
    core = lax.rem(lax.axis_index("pair"), 2)
    me = z * 4 + y

    barrier = pltpu.get_barrier_semaphore()
    for other in range(1, 16):
        pl.semaphore_signal(
            barrier, inc=1, device_id_type=MESH,
            device_id={"z": lax.rem(z + other // 4, 4), "y": lax.rem(y + other % 4, 4)},
        )
    owner_y = [lax.rem(p + 2 * core, 4) for p in range(4)]
    owner = y == lax.rem(z + 2 * core, 4)

    with scope("select"):
        for p in range(4):
            sel[p, 0] = desc[pairs[0, p]]
            col = desc[pairs[1, p]]
            sel[p, 1] = col
            cols[p, z, pl.ds(pl.multiple_of(y * B, B), B), :] = col

        @pl.when(owner)
        def _():
            own[0, 0] = desc[pairs[0, z]]
            own[1, 0] = desc[pairs[1, z]]

    with scope("barrier"):
        pl.semaphore_wait(barrier, 15)

    def to_owner(p, side):
        slot = lax.rem(z + 4 - p, 4) * 4 + lax.rem(y + 4 - owner_y[p], 4)
        recv = (r_recv, c_recv)[side].at[slot]
        return remote(sel.at[p, side], own.at[side, slot], a_send.at[p, side], recv, p, owner_y[p])

    away = [jnp.logical_not((z == p) & (y == owner_y[p])) for p in range(4)]
    with scope("to_owner"):
        for side in (1, 0):
            for p in range(4):
                pl.when(away[p])(lambda p=p: to_owner(p, side).start())

    gather = Gather(cols, g_send, g_recv, z, y)

    def sent():
        for side in (1, 0):
            for p in range(4):
                pl.when(away[p])(lambda p=p: to_owner(p, side).wait_send())

    def pt(number):
        with scope(f"pt{number}"):
            gather.point(number)

    def answer(h):
        dz, dy = NEAR[h]
        return remote(
            stage.at[h], uvr.at[z], u_send.at[h], u_recv.at[z], lax.rem(z + dz, 4), lax.rem(y + dy, 4)
        )

    if not EAGER:
        sent()
    pt(0)
    if EAGER:
        sent()

    @pl.when(jnp.logical_not(owner))
    def _():
        for number in range(1, 5):
            pt(number)

    @pl.when(owner)
    def _():
        def landed(side, slot):
            there = own.at[side, slot]
            remote(there, there, a_send.at[0, 0], (r_recv, c_recv)[side].at[slot], z, y).wait_recv()

        def number_of(slot):
            dz, dy = slot if isinstance(slot, tuple) else (slot // 4, slot % 4)
            return lax.rem(z + dz, 4) * 4 + lax.rem(y + dy, 4)

        na, nb = count_vector(counts, pairs, z, 0), count_vector(counts, pairs, z, 1)
        naf, nbf = na.astype(F32), nb.astype(F32)
        one = 1.0 / (naf + nbf)
        bin_value = jnp.full((1, 128), bins[0], F32)
        mu_bin = nbf * one

        with scope("landed"):
            for slot in range(1, 16):
                landed(1, slot)
            for slot in range(16):
                start = number_of(slot) * B
                kept = lanes() + start < nb
                nus[:, slot * 128 : slot * 128 + 128] = jnp.where(kept, one, 0.0)
                ys[:, slot * 128 : slot * 128 + 128] = jnp.where(kept, 1.0, 0.0)
                kept = lax.broadcasted_iota(jnp.int32, (B, D), 0) + start < jnp.concatenate([nb, nb], axis=1)
                own[1, slot] = own[1, slot] * jnp.where(kept, 1.0, 0.0).astype(BF16)
            nus[:, KP:W] = jnp.where(lanes() == 0, naf * one, 0.0)
            ys[:, KP:W] = jnp.where(lanes() == 0, 1.0, 0.0)

        def multiply(step, raw, tops):
            left = jnp.concatenate([own[0, dz * 4 + dy] for dz, dy in NEAR[2 * step : 2 * step + 2]], axis=0)
            top = jnp.broadcast_to(bin_value * 16.0, (RB, 128))
            for c in range(8):
                right = jnp.concatenate([own[1, 2 * c], own[1, 2 * c + 1]], axis=0)
                part = lax.dot_general(left, right, TRANS, preferred_element_type=F32)
                raw[:, c * 256 : c * 256 + 256] = part
                top = jnp.maximum(top, jnp.maximum(part[:, 0:128], part[:, 128:256]))
            tops[...] = top

        def scale(step, raw, tops):
            rows = slice(step * RB, step * RB + RB)
            top = jnp.max(tops[...], axis=1, keepdims=True) * (LOG2E / 16.0) - SHIFT
            top = jnp.broadcast_to(top, (RB, 128))
            for h in range(2):
                mv[2 * step + h : 2 * step + h + 1, :] = top[h * 128 : h * 128 + 128].T[0:1, :]
            for c in range(CHUNKS):
                at = slice(c * 128, c * 128 + 128)
                if c < 16:
                    value = jnp.exp2(raw[:, at] * (LOG2E / 16.0) - top)
                else:
                    value = jnp.where(lanes() == 0, jnp.exp2(bin_value * LOG2E - top), 0.0)
                kmat[rows, at] = value
                khigh[c, rows, :] = value.astype(BF16)

        with scope("scores"):
            raws = ((raw0, top0), (raw1, top1))
            for step in range(STEPS):
                for dz, dy in NEAR[2 * step : 2 * step + 2]:
                    if dz or dy:
                        landed(0, dz * 4 + dy)
                if step == 2:
                    pt(1)
                if step:
                    scale(step - 1, *raws[(step - 1) % 2])
                multiply(step, *raws[step % 2])
            scale(STEPS - 1, *raws[(STEPS - 1) % 2])

        def weigh(h):
            rows = slice(h * 128, h * 128 + 128)
            total = kmat[rows, 0:128] * ys[:, 0:128]
            for c in range(1, CHUNKS):
                total += kmat[rows, c * 128 : c * 128 + 128] * ys[:, c * 128 : c * 128 + 128]
            return total

        def across(h, total):
            x = one / jnp.sum(total.T, axis=0, keepdims=True)
            xv[h : h + 1, :] = x
            return jnp.where(lanes() + number_of(NEAR[h]) * B < na, x, 0.0)

        def bins_row():
            spread = jnp.sum(ys[...], axis=1, keepdims=True)
            x_bin = mu_bin / jnp.broadcast_to(spread, (1, 128))
            stage[0, 17:18, :] = x_bin
            return x_bin

        def early():
            x_bin = bins_row()
            line = lax.broadcasted_iota(jnp.int32, (16, 128), 0)
            sums = [None] * 9

            def row_step(b):
                halves = []
                for h in (2 * b, 2 * b + 1):
                    x = across(h, weigh(h))
                    high = x.astype(BF16).astype(F32)
                    halves.append(jnp.where(line == 0, high, jnp.where(line == 1, x - high, 0.0)).astype(BF16))
                return jnp.concatenate(halves, axis=1)

            def col_step(b, x):
                rows = slice(b * RB, b * RB + RB)
                for t in range(9):
                    chunks = [khigh[c, rows, :] for c in range(2 * t, min(2 * t + 2, CHUNKS))]
                    part = jnp.dot(x, jnp.concatenate(chunks, axis=1), preferred_element_type=F32)
                    sums[t] = part if b == 0 else sums[t] + part

            x = row_step(0)
            for b in range(1, STEPS):
                after = row_step(b)
                col_step(b - 1, x)
                x = after
            col_step(STEPS - 1, x)
            for t in range(9):
                at = slice(t * 256, min(t * 256 + 256, W))
                both = sums[t][0:1, :] + sums[t][1:2, :]
                ys[:, at] = nus[:, at] / (both + x_bin[:, 0:1])

        def late():
            x_bin = bins_row()

            def row_step(h):
                total = weigh(h)
                across(h, total)
                x = one / jnp.broadcast_to(jnp.sum(total, axis=1, keepdims=True), (B, 128))
                kept = lax.broadcasted_iota(jnp.int32, (B, 128), 0) + number_of(NEAR[h]) * B < na
                xd[h % 2] = jnp.where(kept, x, 0.0)

            sums = [jnp.zeros((8, 128), F32)] * CHUNKS

            def col_step(h):
                for c in range(CHUNKS):
                    part = kmat[h * 128 : h * 128 + 128, c * 128 : c * 128 + 128] * xd[h % 2]
                    sums[c] = sums[c] + jnp.sum(part.reshape(16, 8, 128), axis=0)

            row_step(0)
            for h in range(1, 16):
                row_step(h)
                col_step(h - 1)
            col_step(15)
            for c in range(CHUNKS):
                at = slice(c * 128, c * 128 + 128)
                ys[:, at] = nus[:, at] / (jnp.sum(sums[c], axis=0, keepdims=True) + x_bin)

        def early_sweep(i, _):
            with scope("sweep"):
                early()
            pl.when(i == 0)(lambda: pt(2))
            pl.when(i == 4)(lambda: pt(3))
            return 0

        lax.fori_loop(0, ITERS - EXACT, early_sweep, 0)

        def late_sweep(i, _):
            with scope("exact"):
                late()
            return 0

        lax.fori_loop(0, EXACT, late_sweep, 0)

        with scope("uv"):
            u = jnp.log(xv[...]) - mv[...] * LN2
            u_bin = jnp.log(stage[0, 17:18, :]) - bin_value
            v = [jnp.log(ys[:, c * 128 : c * 128 + 128]) for c in range(16)]
            v_bin = jnp.log(jnp.broadcast_to(ys[:, KP : KP + 1], (1, 128)))
            for h in range(16):
                d = number_of(NEAR[h])
                for c in range(16):
                    stage[h, pl.ds(number_of(c), 1), :] = v[c]
                stage[h, 16:17, :] = u[h : h + 1, :]
                stage[h, 17:18, :] = u_bin
                stage[h, 18:19, :] = v_bin
                stage[h, 19:24, :] = jnp.zeros((5, 128), F32)

            uvr[z] = stage[0]
            for h in range(1, 16):
                answer(h).start()

        pt(4)

    with scope("final"):
        for p in range(4):
            for c in range(8):
                right = cols[p, c // 2, (c % 2) * 256 : (c % 2) * 256 + 256, :]
                part = lax.dot_general(sel[p, 0], right, TRANS, preferred_element_type=F32)
                sv[p, :, c * 256 : c * 256 + 256] = part * 0.0625
            pltpu.make_async_copy(sv.at[p], s_out.at[p], o_sem.at[p]).start()

    with scope("drain"):
        gather.drain()

    with scope("uvwait"):
        for p in range(4):
            def landed(p=p):
                remote(uvr.at[p], uvr.at[p], u_send.at[0], u_recv.at[p], z, y).wait_recv()
            pl.when(away[p])(landed)

    uv_out[...] = uvr[...]

    @pl.when(owner)
    def _():
        for h in range(1, 16):
            answer(h).wait_send()

    for p in range(4):
        pltpu.make_async_copy(sv.at[p], s_out.at[p], o_sem.at[p]).wait()


def last_kernel(pairs, counts, bins, s, uv, out, row_out, col_out):
    p = pl.program_id(0)
    start = (lax.axis_index("z") * 4 + lax.axis_index("y")) * B
    na, nb = count_vector(counts, pairs, p, 0), count_vector(counts, pairs, p, 1)
    norm = -jnp.log((na + nb).astype(F32))
    bin_value = jnp.full((1, 128), bins[0], F32)
    u = uv[p, 16:17, :]
    row_kept = lanes() + start < na
    u_down = jnp.broadcast_to(u, (B, 128)).T
    kept = lax.broadcasted_iota(jnp.int32, (B, 128), 0) + start < na
    for c in range(16):
        at = slice(c * 128, c * 128 + 128)
        v = uv[p, c : c + 1, :]
        col_kept = lanes() + c * 128 < nb
        out[0, :, at] = jnp.where(kept & col_kept, s[0, :, at] + u_down + v - norm, 0.0)

    def bin_lines(q):
        row_out[q : q + 1, :] = jnp.where(row_kept, bin_value + u + uv[p, 18:19, :] - norm, 0.0)
        for c in range(16):
            line = bin_value + uv[p, 17:18, :] + uv[p, c : c + 1, :] - norm
            col_out[q : q + 1, c * 128 : c * 128 + 128] = jnp.where(lanes() + c * 128 < nb, line, 0.0)

    for q in range(4):
        pl.when(p == q)(lambda q=q: bin_lines(q))


def on_device(descriptors, counts, pairs, bin_score):
    smem = pl.BlockSpec(memory_space=pltpu.SMEM)
    vmem = pl.BlockSpec(memory_space=pltpu.VMEM)
    dma = pltpu.SemaphoreType.DMA
    s, uv = pl.pallas_call(
        main_kernel,
        out_shape=(
            jax.ShapeDtypeStruct((4, B, KP), F32),
            jax.ShapeDtypeStruct((4, UVROWS, 128), F32),
        ),
        in_specs=[smem, smem, smem, vmem],
        out_specs=(pl.BlockSpec(memory_space=pl.ANY), vmem),
        scratch_shapes=[
            pltpu.VMEM((4, 2, B, D), BF16),
            pltpu.VMEM((2, 16, B, D), BF16),
            pltpu.VMEM((4, 4, 4 * B, D), BF16),
            pltpu.VMEM((KP, W), F32),
            pltpu.VMEM((CHUNKS, KP, 128), BF16),
            pltpu.VMEM((RB, KP), F32),
            pltpu.VMEM((RB, KP), F32),
            pltpu.VMEM((RB, 128), F32),
            pltpu.VMEM((RB, 128), F32),
            pltpu.VMEM((1, W), F32),
            pltpu.VMEM((1, W), F32),
            pltpu.VMEM((2, B, 128), F32),
            pltpu.VMEM((16, 128), F32),
            pltpu.VMEM((16, 128), F32),
            pltpu.VMEM((16, UVROWS, 128), F32),
            pltpu.VMEM((4, UVROWS, 128), F32),
            pltpu.VMEM((4, B, KP), F32),
            dma((4, 2)), dma((16,)), dma((16,)), dma((28,)), dma((28,)), dma((16,)), dma((4,)), dma((4,)),
        ],
        compiler_params=pltpu.CompilerParams(
            collective_id=0, has_side_effects=True, vmem_limit_bytes=60 * 1024 * 1024
        ),
        name="match",
    )(pairs.T, counts, bin_score, descriptors)
    return pl.pallas_call(
        last_kernel,
        grid=(4,),
        out_shape=(
            jax.ShapeDtypeStruct((4, B, KP), F32),
            jax.ShapeDtypeStruct((4, B), F32),
            jax.ShapeDtypeStruct((4, KP), F32),
        ),
        in_specs=[
            smem, smem, smem,
            pl.BlockSpec((1, B, KP), lambda p: (p, 0, 0)),
            pl.BlockSpec((4, UVROWS, 128), lambda p: (0, 0, 0)),
        ],
        out_specs=(
            pl.BlockSpec((1, B, KP), lambda p: (p, 0, 0)),
            pl.BlockSpec((4, B), lambda p: (0, 0)),
            pl.BlockSpec((4, KP), lambda p: (0, 0)),
        ),
        name="assign",
    )(pairs.T, counts, bin_score, s, uv)


def solution(mesh):
    finer = Mesh(mesh.devices.reshape(mesh.shape["pair"], 4, 4), ("pair", "z", "y"))
    row = ("z", "y")
    return jax.shard_map(
        on_device,
        mesh=finer,
        in_specs=(P("pair", row, None), P("pair"), P("pair", None), P()),
        out_specs=(P("pair", row, None), P("pair", row), P("pair", None)),
        check_vma=False,
    )
```

time: 86.5 us -> 67.4 us (0.78)
  Pallas kernels: 83.6 us -> 65.9 us
  local copies, waits for them, and re-layouts: 1.34 us -> 0 us
    pallas_call x1, Pallas kernels: 78.4 us -> 60.8 us  [on_device(): pl.pallas_call(main_kernel, out_shape=(jax.ShapeDtypeStruct((4, B, KP), F...]
    unnamed x1 -> x0, local copies, waits for them, and re-layouts: 1.34 us -> none
where the time goes in v2:
time: 67.4 us; the launch traced here: 67.2 us
  Pallas kernels  65.9 us (98%)
  between operations  1.28 us (2%)
    pallas_call x1, Pallas kernels, on_device(): pl.pallas_call(main_kernel, out_shape=(jax.ShapeDtypeStruct((4, B, KP), F...  60.8 us
    pallas_call x1, Pallas kernels, on_device(): pl.pallas_call(last_kernel, grid=(4,), out_shape=(jax.ShapeDtypeStruct((4...  5.15 us

profile of v2, /device:TPU:0, one launch (start us, length us, event | category | flops | bytes accessed | tf_op | source)
XLA Modules:
  0.0 67.2 jit_solution(4688519367292308298)
XLA Ops:
  1.3 60.8 %match.1 = (f32[4,128,2048]{2,1,0:T(8,128)}, f32[4,24,128]{2,1,0:T(8,128)}) custom-call(s32[2,4]{1,0:T(2,128)} %bitcast.1, s32[8]{0:T(128)} %counts.3, f32[1]{0:T(128)S(6)} %copy.7.bins, bf16[8,128,256]{2,1,0:T(8,128)(2,1)} %desc.1), custom_call_target="tpu_custom_call" | custom-call | tf_op jit(solution)/shard_map/match/pallas_call | solution.py:448
  62.0 5.1 %assign.1 = (f32[4,128,2048]{2,1,0:T(8,128)}, f32[4,128]{1,0:T(4,128)}, f32[4,2048]{1,0:T(4,128)}) custom-call(s32[2,4]{1,0:T(2,128)} %bitcast.2, s32[8]{0:T(128)} %counts.3, f32[1]{0:T(128)S(6)} %copy.7.bins, f32[4,128,2048]{2,1,0:T(8,128)} %get-tuple-element.5.s, f32[4,24,128]{2,1,0:T(8,128)} %get-tuple-element.6.uv), custom_call_target="tpu_custom_call" | custom-call | tf_op jit(solution)/shard_map/assign/pallas_call | solution.py:481
